TPU v7x, 128 devices: a whole 4x4x4 slice. The times are simulated.
128 devices in a mesh: row: 16 (over y, z_lo, core), col: 8 (over z_hi, x).
Axes of the slice: x: 4, y: 4, z: 4 (z_hi: 2, z_lo: 2; z = z_hi * 2 + z_lo), core: 2. Of those that a mesh axis runs over, the one named last changes fastest.
Arguments:
- points: float32 [64, 32768], P(None, ('row', 'col')), may hold values from -6 to 6
- labels: int32 [256], P(('row', 'col')), may hold values from 0 to 1
- solution: float32 [32768], P(('row', 'col')), may hold values from -6 to 6
- residual: float32 [32768], P(('row', 'col')), may hold values from -6 to 6
- direction: float32 [32768], P(('row', 'col')), may hold values from -6 to 6
- len_low: float32 [64], replicated, may hold values from 0.75 to 40
- len_high: float32 [64], replicated, may hold values from 0.9 to 40
- variances: float32 [2], replicated, may hold values from 0.5 to 2
- nugget: float32 [2], replicated, may hold values from 0.3 to 1.5
- coupling: float32 [1], replicated, may hold values from 0.6 to 1.6
Outputs:
- solution_next: float32 [32768], P(('row', 'col'))
- residual_next: float32 [32768], P(('row', 'col'))
- direction_next: float32 [32768], P(('row', 'col'))
All inputs are finite; a program needn't handle non-finite values.
Results may differ from a plain program's by a relative error of at most 0.00027.
Values sent between devices are 32-bit elements; how exact they have to be, the bound alone decides.
A program may use at most 64 MiB of HBM per device.

v0:
```python
import functools

import jax
import jax.numpy as jnp
from jax import lax
from jax.sharding import Mesh
from jax.sharding import PartitionSpec as P

COL = ("col_0", "col_1")
ROW = ("row_0", "row_1", "row_2")
ROW_COL = ("row_0", "row_1", "row_2", "col_0", "col_1")


def in_one_piece(arrays, axis, dim, along):
    widths = [a.shape[along] for a in arrays]
    both = jnp.concatenate(arrays, axis=along)
    whole = lax.all_gather(both, axis, axis=dim, tiled=True)
    return tuple(jnp.split(whole, [sum(widths[:k]) for k in range(1, len(widths))], axis=along))


def laid_out(blocks, dim):
    blocks = jnp.moveaxis(blocks, 0, dim)
    shape = blocks.shape
    return blocks.reshape(*shape[:dim], shape[dim] * shape[dim + 1], *shape[dim + 2 :])


def copy_for_each(x, axis):
    length = lax.axis_size(axis)
    return lax.all_to_all(jnp.broadcast_to(x[None], (length, *x.shape)), axis, 0, 0, tiled=True)


def gather_directly(x, axis, dim):
    return laid_out(copy_for_each(x, axis), dim)


def sent_together(arrays, axis, dim, along):
    ends, at = ([], 0)
    for a in arrays[:-1]:
        at += a.shape[along]
        ends.append(at)
    both = jnp.concatenate(arrays, axis=along)
    return tuple(jnp.split(gather_directly(both, axis, dim), ends, axis=along))


def split_up(x, dim, length):
    before, after = (x.shape[:dim], x.shape[dim + 1 :])
    return jnp.moveaxis(x.reshape(*before, length, -1, *after), dim, 0)


def sent_and_summed(x, axis, dim):
    blocks = split_up(x, dim, lax.axis_size(axis))
    arrived = lax.all_to_all(blocks, axis, split_axis=0, concat_axis=0, tiled=True)
    return arrived.sum(axis=0)


def one_axis_at_a_time(x, axes):
    return functools.reduce(lax.psum, axes, x)


def scale_factors(fidelity, coupling):
    return 1.0 + (coupling[0] - 1.0) * fidelity


def kernel_terms(
    totals,
    rows_low,
    rows_high,
    norms_low,
    norms_high,
    col_low,
    col_high,
    col_label,
    col_dir,
    coupling,
):
    col_width = col_low.shape[1]
    block_width = col_width
    while block_width > 1024 and block_width % 2 == 0:
        block_width = block_width // 2
    dims = (((0,), (0,)), ((), ()))

    def one_block(block_index, accumulated):
        offset = block_index * block_width
        part_low = lax.dynamic_slice_in_dim(col_low, offset, block_width, 1)
        part_high = lax.dynamic_slice_in_dim(col_high, offset, block_width, 1)
        part_label = lax.dynamic_slice_in_dim(col_label, offset, block_width, 1)[0]
        part_dir = lax.dynamic_slice_in_dim(col_dir, offset, block_width, 1)[0]
        part_nlow = jnp.sum(part_low * part_low, 0)
        part_nhigh = jnp.sum(part_high * part_high, 0)
        dist_low = (
            norms_low[:, None]
            + part_nlow[None, :]
            - 2.0 * lax.dot_general(rows_low, part_low, dims, precision=lax.Precision.HIGHEST)
        )
        dist_high = (
            norms_high[:, None]
            + part_nhigh[None, :]
            - 2.0 * lax.dot_general(rows_high, part_high, dims, precision=lax.Precision.HIGHEST)
        )
        weights_low = scale_factors(part_label, coupling) * part_dir
        weights_high = part_label * part_dir
        next_low = accumulated[0] + jnp.dot(
            jnp.exp(-0.5 * dist_low), weights_low, precision=lax.Precision.HIGHEST
        )
        next_high = accumulated[1] + jnp.dot(
            jnp.exp(-0.5 * dist_high), weights_high, precision=lax.Precision.HIGHEST
        )
        return (next_low, next_high)

    return lax.fori_loop(0, col_width // block_width, one_block, totals)


def body(
    points, labels, solution, residual, direction, len_low, len_high, variances, nugget, coupling
):
    own_label = jnp.repeat(labels, 128).astype(jnp.float32)
    label_row = own_label[None, :]
    dir_row = direction[None, :]
    rows_points, rows_label = in_one_piece((points, label_row), COL, 1, 0)
    rows_low = rows_points / len_low[:, None]
    rows_high = rows_points / len_high[:, None]
    norms_low = jnp.sum(rows_low * rows_low, 0)
    norms_high = jnp.sum(rows_high * rows_high, 0)
    zeros_rows = jnp.zeros((rows_low.shape[1],), jnp.float32)
    pieces = sent_together((points, label_row, dir_row), ROW, 1, 0)
    sum_low, sum_high = kernel_terms(
        (zeros_rows, zeros_rows),
        rows_low,
        rows_high,
        norms_low,
        norms_high,
        pieces[0] / len_low[:, None],
        pieces[0] / len_high[:, None],
        pieces[1],
        pieces[2],
        coupling,
    )
    rows_fidelity = rows_label[0]
    row_terms = (
        variances[0] * scale_factors(rows_fidelity, coupling) * sum_low
        + variances[1] * rows_fidelity * sum_high
    )
    own_terms = sent_and_summed(row_terms, COL, 0)
    nugget_points = nugget[0] + (nugget[1] - nugget[0]) * own_label
    kernel_image = own_terms + nugget_points * direction
    old_norm, curvature, cross_term, image_norm = (
        one_axis_at_a_time(jnp.sum(residual * residual), ROW_COL),
        one_axis_at_a_time(jnp.sum(direction * kernel_image), ROW_COL),
        one_axis_at_a_time(jnp.sum(residual * kernel_image), ROW_COL),
        one_axis_at_a_time(jnp.sum(kernel_image * kernel_image), ROW_COL),
    )
    step_size = old_norm / curvature
    solution_next = solution + step_size * direction
    residual_next = residual - step_size * kernel_image
    new_norm = old_norm - 2.0 * step_size * cross_term + step_size * step_size * image_norm
    direction_next = residual_next + new_norm / old_norm * direction
    return (solution_next, residual_next, direction_next)


def solution(mesh):
    torus = Mesh(mesh.devices.reshape(4, 2, 2, 2, 4), ("row_0", "row_1", "row_2", "col_0", "col_1"))
    in_specs = (
        P(None, ROW_COL),
        P(ROW_COL),
        P(ROW_COL),
        P(ROW_COL),
        P(ROW_COL),
        P(),
        P(),
        P(),
        P(),
        P(),
    )
    out_specs = (P(ROW_COL), P(ROW_COL), P(ROW_COL))
    return jax.shard_map(body, mesh=torus, in_specs=in_specs, out_specs=out_specs, check_vma=False)
```

profile of v0, /device:TPU:1, one launch (start us, length us, event | category | flops | bytes accessed | tf_op | source)
XLA Modules:
  0.0 211.8 jit_solution(11609736806748778649)
XLA Ops:
  0.6 0.0 copy-start.2
  0.6 0.0 copy-start.3
  0.7 0.7 convert_element_type.16
  1.3 0.1 broadcast_in_dim.34
  1.4 0.9 pad_maximum_fusion.1
  2.3 1.1 broadcast_in_dim.37
  3.3 7.3 %all-to-all-start = ((f32[16,66,256]{2,1,0:T(8,128)}), f32[16,66,256]{2,1,0:T(8,128)S(1)}, u32[]{:S(2)}, u32[]{:S(2)}) async-start(f32[16,66,256]{2,1,0:T(8,128)} %broadcast_in_dim.37), calls=%async_computation | async-start | bytes 2359296 | tf_op jit(solution)/shard_map/all_to_all | solution.py:29
  10.7 0.8 pad_maximum_fusion
  12.2 1.3 fusion.34
  14.8 1.3 fusion.35
  16.1 31.1 %all_gather.3 = f32[65,2048]{1,0:T(8,128)S(1)} all-gather(f32[65,256]{1,0:T(8,128)S(1)} %pad_maximum_fusion), channel_id=1, replica_groups=mesh['row_0'=4,'row_1'=2,'row_2'=2,'col_0'=2,'col_1'=4] {'col_0','col_1'}, dimensions={1}, use_global_device_ids=true | all-gather | bytes 599040 | tf_op jit(solution)/shard_map/all_gather | solution.py:17
  47.1 0.9 multiply_reduce_fusion.2
  48.0 1.3 add_multiply_fusion.1
  49.4 0.1 slice_bitcast_fusion
  49.5 0.1 copy.18
  49.6 0.3 broadcast_divide_fusion
  50.0 102.7 %while.18 = (s32[]{:T(128)}, f32[2048]{0:T(1024)S(1)}, f32[2048]{0:T(1024)S(1)}, f32[2048]{0:T(1024)S(1)}, f32[64,4096]{1,0:T(8,128)S(1)}, /*index=5*/f32[64,204...) while((s32[]{:T(128)}, f32[2048]{0:T(1024)S(1)}, ...), condition=%wide.region_11.0_spmd.clone, body=%wide.region_8.11_spmd.clone.sunk | while | flops 3288606720 | bytes 35791080 | solution.py:110
  50.0 6.7 %fusion.62 = f32[1024,2048]{1,0:T(8,128)S(1)} fusion(f32[64,2048]{1,0:T(8,128)S(1)} %get-tuple-element.517, f32[64,4096]{1,0:T(8,128)S(1)} %get-tuple-element.516, s32[]{:T(128)S(6)} %select_n.14), kind=kOutput, calls=%fused_computation.24.clone.1 | convolution fusion | flops 1610612736 | bytes 9175044 | tf_op jit(solution)/shard_map/while/body/eval_jaxpr/dot_general | solution.py:93
  56.8 0.1 multiply_reduce_fusion.9
  56.8 6.0 %fusion.63 = f32[1,2048]{1,0:T(1,128)S(1)} fusion(f32[1024,1]{0,1:T(1,128)S(1)} %bitcast.77, f32[1024,2048]{1,0:T(8,128)S(1)} %fusion.62, f32[1024]{0:T(1024)S(1)} %get-tuple-element.477, f32[2048]{0:T(1024)S(1)} %get-tuple-element.515), kind=kOutput, calls=%fused_computation.7.clone.1 | convolution fusion | flops 33554432 | bytes 8413184 | tf_op jit(solution)/shard_map/while/body/eval_jaxpr/dot_general | solution.py:102
  62.9 6.7 %fusion.64 = f32[1024,2048]{1,0:T(8,128)S(1)} fusion(f32[64,2048]{1,0:T(8,128)S(1)} %get-tuple-element.523, f32[64,4096]{1,0:T(8,128)S(1)} %get-tuple-element.522, s32[]{:T(128)S(6)} %select_n.14), kind=kOutput, calls=%fused_computation.22.clone.1 | convolution fusion | flops 1610612736 | bytes 9175044 | tf_op jit(solution)/shard_map/while/body/eval_jaxpr/dot_general | solution.py:98
  69.6 6.0 %fusion.65 = f32[1,2048]{1,0:T(1,128)S(1)} fusion(f32[1024,1]{0,1:T(1,128)S(1)} %bitcast.76, f32[1024,2048]{1,0:T(8,128)S(1)} %fusion.64, f32[1024]{0:T(1024)S(1)} %get-tuple-element.479, f32[2048]{0:T(1024)S(1)} %get-tuple-element.521), kind=kOutput, calls=%fused_computation.3.clone.1 | convolution fusion | flops 33554432 | bytes 8413184 | tf_op jit(solution)/shard_map/while/body/eval_jaxpr/dot_general | solution.py:105
  75.7 6.7 %fusion.62 = f32[1024,2048]{1,0:T(8,128)S(1)} fusion(f32[64,2048]{1,0:T(8,128)S(1)} %get-tuple-element.517, f32[64,4096]{1,0:T(8,128)S(1)} %get-tuple-element.516, s32[]{:T(128)S(6)} %select_n.14), kind=kOutput, calls=%fused_computation.24.clone.1 | convolution fusion | flops 1610612736 | bytes 9175044 | tf_op jit(solution)/shard_map/while/body/eval_jaxpr/dot_general | solution.py:93
  82.4 0.1 multiply_reduce_fusion.9
  82.5 6.0 %fusion.63 = f32[1,2048]{1,0:T(1,128)S(1)} fusion(f32[1024,1]{0,1:T(1,128)S(1)} %bitcast.77, f32[1024,2048]{1,0:T(8,128)S(1)} %fusion.62, f32[1024]{0:T(1024)S(1)} %get-tuple-element.477, f32[2048]{0:T(1024)S(1)} %get-tuple-element.515), kind=kOutput, calls=%fused_computation.7.clone.1 | convolution fusion | flops 33554432 | bytes 8413184 | tf_op jit(solution)/shard_map/while/body/eval_jaxpr/dot_general | solution.py:102
  88.5 6.7 %fusion.64 = f32[1024,2048]{1,0:T(8,128)S(1)} fusion(f32[64,2048]{1,0:T(8,128)S(1)} %get-tuple-element.523, f32[64,4096]{1,0:T(8,128)S(1)} %get-tuple-element.522, s32[]{:T(128)S(6)} %select_n.14), kind=kOutput, calls=%fused_computation.22.clone.1 | convolution fusion | flops 1610612736 | bytes 9175044 | tf_op jit(solution)/shard_map/while/body/eval_jaxpr/dot_general | solution.py:98
  95.3 6.0 %fusion.65 = f32[1,2048]{1,0:T(1,128)S(1)} fusion(f32[1024,1]{0,1:T(1,128)S(1)} %bitcast.76, f32[1024,2048]{1,0:T(8,128)S(1)} %fusion.64, f32[1024]{0:T(1024)S(1)} %get-tuple-element.479, f32[2048]{0:T(1024)S(1)} %get-tuple-element.521), kind=kOutput, calls=%fused_computation.3.clone.1 | convolution fusion | flops 33554432 | bytes 8413184 | tf_op jit(solution)/shard_map/while/body/eval_jaxpr/dot_general | solution.py:105
  101.4 6.7 %fusion.62 = f32[1024,2048]{1,0:T(8,128)S(1)} fusion(f32[64,2048]{1,0:T(8,128)S(1)} %get-tuple-element.517, f32[64,4096]{1,0:T(8,128)S(1)} %get-tuple-element.516, s32[]{:T(128)S(6)} %select_n.14), kind=kOutput, calls=%fused_computation.24.clone.1 | convolution fusion | flops 1610612736 | bytes 9175044 | tf_op jit(solution)/shard_map/while/body/eval_jaxpr/dot_general | solution.py:93
  108.1 0.1 multiply_reduce_fusion.9
  108.2 6.0 %fusion.63 = f32[1,2048]{1,0:T(1,128)S(1)} fusion(f32[1024,1]{0,1:T(1,128)S(1)} %bitcast.77, f32[1024,2048]{1,0:T(8,128)S(1)} %fusion.62, f32[1024]{0:T(1024)S(1)} %get-tuple-element.477, f32[2048]{0:T(1024)S(1)} %get-tuple-element.515), kind=kOutput, calls=%fused_computation.7.clone.1 | convolution fusion | flops 33554432 | bytes 8413184 | tf_op jit(solution)/shard_map/while/body/eval_jaxpr/dot_general | solution.py:102
  114.2 6.7 %fusion.64 = f32[1024,2048]{1,0:T(8,128)S(1)} fusion(f32[64,2048]{1,0:T(8,128)S(1)} %get-tuple-element.523, f32[64,4096]{1,0:T(8,128)S(1)} %get-tuple-element.522, s32[]{:T(128)S(6)} %select_n.14), kind=kOutput, calls=%fused_computation.22.clone.1 | convolution fusion | flops 1610612736 | bytes 9175044 | tf_op jit(solution)/shard_map/while/body/eval_jaxpr/dot_general | solution.py:98
  121.0 6.0 %fusion.65 = f32[1,2048]{1,0:T(1,128)S(1)} fusion(f32[1024,1]{0,1:T(1,128)S(1)} %bitcast.76, f32[1024,2048]{1,0:T(8,128)S(1)} %fusion.64, f32[1024]{0:T(1024)S(1)} %get-tuple-element.479, f32[2048]{0:T(1024)S(1)} %get-tuple-element.521), kind=kOutput, calls=%fused_computation.3.clone.1 | convolution fusion | flops 33554432 | bytes 8413184 | tf_op jit(solution)/shard_map/while/body/eval_jaxpr/dot_general | solution.py:105
  127.1 6.7 %fusion.62 = f32[1024,2048]{1,0:T(8,128)S(1)} fusion(f32[64,2048]{1,0:T(8,128)S(1)} %get-tuple-element.517, f32[64,4096]{1,0:T(8,128)S(1)} %get-tuple-element.516, s32[]{:T(128)S(6)} %select_n.14), kind=kOutput, calls=%fused_computation.24.clone.1 | convolution fusion | flops 1610612736 | bytes 9175044 | tf_op jit(solution)/shard_map/while/body/eval_jaxpr/dot_general | solution.py:93
  133.8 0.1 multiply_reduce_fusion.9
  133.9 6.0 %fusion.63 = f32[1,2048]{1,0:T(1,128)S(1)} fusion(f32[1024,1]{0,1:T(1,128)S(1)} %bitcast.77, f32[1024,2048]{1,0:T(8,128)S(1)} %fusion.62, f32[1024]{0:T(1024)S(1)} %get-tuple-element.477, f32[2048]{0:T(1024)S(1)} %get-tuple-element.515), kind=kOutput, calls=%fused_computation.7.clone.1 | convolution fusion | flops 33554432 | bytes 8413184 | tf_op jit(solution)/shard_map/while/body/eval_jaxpr/dot_general | solution.py:102
  139.9 6.7 %fusion.64 = f32[1024,2048]{1,0:T(8,128)S(1)} fusion(f32[64,2048]{1,0:T(8,128)S(1)} %get-tuple-element.523, f32[64,4096]{1,0:T(8,128)S(1)} %get-tuple-element.522, s32[]{:T(128)S(6)} %select_n.14), kind=kOutput, calls=%fused_computation.22.clone.1 | convolution fusion | flops 1610612736 | bytes 9175044 | tf_op jit(solution)/shard_map/while/body/eval_jaxpr/dot_general | solution.py:98
  146.7 6.0 %fusion.65 = f32[1,2048]{1,0:T(1,128)S(1)} fusion(f32[1024,1]{0,1:T(1,128)S(1)} %bitcast.76, f32[1024,2048]{1,0:T(8,128)S(1)} %fusion.64, f32[1024]{0:T(1024)S(1)} %get-tuple-element.479, f32[2048]{0:T(1024)S(1)} %get-tuple-element.521), kind=kOutput, calls=%fused_computation.3.clone.1 | convolution fusion | flops 33554432 | bytes 8413184 | tf_op jit(solution)/shard_map/while/body/eval_jaxpr/dot_general | solution.py:105
  152.7 0.6 multiply_add_fusion
  153.3 5.3 %all-to-all-start.1 = ((f32[8,1,256]{2,1,0:T(1,128)}), f32[8,1,256]{2,1,0:T(1,128)S(1)}, u32[]{:S(2)}, u32[]{:S(2)}) async-start(f32[8,1,256]{2,1,0:T(1,128)} %bitcast.10), calls=%async_computation.1 | async-start | bytes 16384 | tf_op jit(solution)/shard_map/all_to_all | solution.py:52
  158.6 0.6 multiply_add_fusion.3
  159.2 5.9 %all-to-all-done.1 = f32[8,1,256]{2,1,0:T(1,128)S(1)} async-done(((f32[8,1,256]{2,1,0:T(1,128)}), f32[8,1,256]{2,1,0:T(1,128)S(1)}, u32[]{:S(2)}, u32[]{:S(2)}) %all-to-all-start.1) | async-done | bytes 8224 | tf_op jit(solution)/shard_map/all_to_all | solution.py:52
  165.2 0.7 multiply_reduce_fusion.4
  165.9 9.6 %all-reduce.1 = (f32[]{:T(128)}, f32[]{:T(128)}, f32[]{:T(128)}, f32[]{:T(128)}) all-reduce(f32[]{:T(128)} %get-tuple-element.323, f32[]{:T(128)} %get-tuple-element.324, f32[]{:T(128)} %get-tuple-element.322, f32[]{:T(128)} %get-tuple-element.321), channel_id=1, replica_groups=mesh['row_0'=4,'row_1'=2,'row_2'=2,'col_0'=2,'col_1'=4] {'row_0'}, use_global_device_ids=true, to_apply=%region_1.0 | all-reduce | flops 4 | bytes 32 | tf_op jit(solution)/shard_map/psum | solution.py:57
  175.4 4.4 %all-reduce.4 = (f32[]{:T(128)}, f32[]{:T(128)}, f32[]{:T(128)}, f32[]{:T(128)}) all-reduce(f32[]{:T(128)} %get-tuple-element.353, f32[]{:T(128)} %get-tuple-element.354, f32[]{:T(128)} %get-tuple-element.355, f32[]{:T(128)} %get-tuple-element.356), channel_id=1, replica_groups=mesh['row_0'=4,'row_1'=2,'row_2'=2,'col_0'=2,'col_1'=4] {'row_1'}, use_global_device_ids=true, to_apply=%region_2.3 | all-reduce | flops 4 | bytes 32 | tf_op jit(solution)/shard_map/psum | solution.py:57
  179.8 13.9 %all-reduce.3 = (f32[]{:T(128)}, f32[]{:T(128)}, f32[]{:T(128)}, f32[]{:T(128)}) all-reduce(f32[]{:T(128)} %get-tuple-element.365, f32[]{:T(128)} %get-tuple-element.366, f32[]{:T(128)} %get-tuple-element.367, f32[]{:T(128)} %get-tuple-element.368), channel_id=1, replica_groups=mesh['row_0'=4,'row_1'=2,'row_2'=2,'col_0'=2,'col_1'=4] {'row_2'}, use_global_device_ids=true, to_apply=%region_3.4 | all-reduce | flops 4 | bytes 32 | tf_op jit(solution)/shard_map/psum | solution.py:57
  193.8 5.9 %all-reduce.2 = (f32[]{:T(128)}, f32[]{:T(128)}, f32[]{:T(128)}, f32[]{:T(128)}) all-reduce(f32[]{:T(128)} %get-tuple-element.361, f32[]{:T(128)} %get-tuple-element.362, f32[]{:T(128)} %get-tuple-element.363, f32[]{:T(128)} %get-tuple-element.364), channel_id=1, replica_groups=mesh['row_0'=4,'row_1'=2,'row_2'=2,'col_0'=2,'col_1'=4] {'col_0'}, use_global_device_ids=true, to_apply=%region_4.5 | all-reduce | flops 4 | bytes 32 | tf_op jit(solution)/shard_map/psum | solution.py:57
  199.7 7.6 %all-reduce = (f32[]{:T(128)}, f32[]{:T(128)}, f32[]{:T(128)}, f32[]{:T(128)}) all-reduce(f32[]{:T(128)} %get-tuple-element.357, f32[]{:T(128)} %get-tuple-element.358, f32[]{:T(128)} %get-tuple-element.359, f32[]{:T(128)} %get-tuple-element.360), channel_id=1, replica_groups=mesh['row_0'=4,'row_1'=2,'row_2'=2,'col_0'=2,'col_1'=4] {'col_1'}, use_global_device_ids=true, to_apply=%region_5.0 | all-reduce | flops 4 | bytes 32 | tf_op jit(solution)/shard_map/psum | solution.py:57
  211.3 0.6 multiply_add_fusion.1
  (31 shorter events, 0.2 us)
Async XLA Ops:
  0.6 49.0 %copy-start.2 = (f32[64]{0:T(128)S(1)}, f32[64]{0:T(128)}, u32[]{:S(2)}) copy-start(f32[64]{0:T(128)} %param.18) | copy-start | bytes 772
  0.6 49.0 %copy-start.3 = (f32[64]{0:T(128)S(1)}, f32[64]{0:T(128)}, u32[]{:S(2)}) copy-start(f32[64]{0:T(128)} %param.17) | copy-start | bytes 772
  3.3 46.0 %all-to-all-start = ((f32[16,66,256]{2,1,0:T(8,128)}), f32[16,66,256]{2,1,0:T(8,128)S(1)}, u32[]{:S(2)}, u32[]{:S(2)}) async-start(f32[16,66,256]{2,1,0:T(8,128)} %broadcast_in_dim.37), calls=%async_computation | async-start | bytes 2359296 | tf_op jit(solution)/shard_map/all_to_all | solution.py:29
  49.9 108.7 %copy-start.5 = (s32[2]{0:T(128)S(1)}, s32[2]{0:T(128)}, u32[]{:S(2)}) copy-start(s32[2]{0:T(128)} %param.13) | copy-start | bytes 28
  49.9 115.3 %copy-start = (f32[256]{0:T(256)S(1)}, f32[256]{0:T(256)}, u32[]{:S(2)}) copy-start(f32[256]{0:T(256)} %param.16) | copy-start | bytes 3076
  49.9 115.3 %copy-start.1 = (f32[256]{0:T(256)S(1)}, f32[256]{0:T(256)}, u32[]{:S(2)}) copy-start(f32[256]{0:T(256)} %param.15) | copy-start | bytes 3076
  49.9 161.3 %copy-start.4 = (f32[256]{0:T(256)S(1)}, f32[256]{0:T(256)}, u32[]{:S(2)}) copy-start(f32[256]{0:T(256)} %param.14) | copy-start | bytes 3076
  153.3 11.9 %all-to-all-start.1 = ((f32[8,1,256]{2,1,0:T(1,128)}), f32[8,1,256]{2,1,0:T(1,128)S(1)}, u32[]{:S(2)}, u32[]{:S(2)}) async-start(f32[8,1,256]{2,1,0:T(1,128)} %bitcast.10), calls=%async_computation.1 | async-start | bytes 16384 | tf_op jit(solution)/shard_map/all_to_all | solution.py:52
where the time goes:
time: 215 us; the launch traced here: 212 us
  matrix products  102 us (47%)
  blocking collectives  72.4 us (34%)
  starting transfers between devices  12.6 us (6%)
  other arithmetic  7.73 us (4%)
  between operations  6.72 us (3%)
  waiting for transfers between devices  5.92 us (3%)
  local copies, waits for them, and re-layouts  4.07 us (2%)
    psum x5, blocking collectives, one_axis_at_a_time(): return functools.reduce(lax.psum, axes, x)  41.4 us
    all_gather x1, blocking collectives, in_one_piece(): whole = lax.all_gather(both, axis, axis=dim, tiled=True)  31.1 us
    dot_general x4, matrix products, one_block(): lax.dot_general(rows_high, part_high, dims, precision=lax.Precision.HIGHEST)  27 us
    dot_general x4, matrix products, one_block(): lax.dot_general(rows_low, part_low, dims, precision=lax.Precision.HIGHEST)  26.9 us
    dot_general x4, matrix products, one_block(): jnp.dot(jnp.exp(-0.5 * dist_high), weights_high, precision=lax.Precision....  24.1 us
    dot_general x4, matrix products, one_block(): jnp.dot(jnp.exp(-0.5 * dist_low), weights_low, precision=lax.Precision.HI...  24.1 us
    all_to_all x1, starting transfers between devices, copy_for_each(): lax.all_to_all(jnp.broadcast_to(x[None], (length, *x.shape)), axis, 0, 0,...  7.33 us
    all_to_all x1, waiting for transfers between devices, sent_and_summed(): lax.all_to_all(blocks, axis, split_axis=0, concat_axis=0, tiled=True)  5.91 us
  transfers between devices with their start and end apart: 2, of which 1 were waited for; matrix products, arithmetic and copies ran while one was open for 3% of the time, Pallas kernels for 0%

commit v1 on v0

v1 whole, which is shorter than its diff:
```python
import functools
import itertools
import math

import jax
import jax.numpy as jnp
from jax import lax
from jax.experimental import pallas as pl
from jax.experimental.pallas import tpu as pltpu
from jax.sharding import PartitionSpec as P

MESH = pl.DeviceIdType.MESH
F32 = jnp.float32
BF16 = jnp.bfloat16
LOG2E = math.log2(math.e)
MASKED = -2000.0
WIDTH = 256
ROWS = 72

OFFSETS = [
    (0, 0, 0, 0),
    (1, 0, 0, 0),
    (0, 0, -1, 0),
    (0, 1, 0, 1),
    (-1, 0, 0, 1),
    (0, -1, -1, 1),
    (0, 1, 1, 0),
    (-1, 0, -1, 1),
    (-1, 1, 0, 1),
    (1, -1, 1, 0),
    (1, -1, 1, 1),
    (-1, -1, -1, 1),
    (-1, -1, 1, 0),
    (1, 1, -1, 1),
    (1, 1, 1, 1),
]
SOURCE = {s: (OFFSETS[s], 0) for s in range(1, len(OFFSETS))}
SEND_ORDER = [14, 13, 12, 11, 10, 9, 8, 7, 6, 5, 4, 3, 2, 1]
ARRIVAL = [0, 14, 13, 12, 11, 10, 9, 8, 7, 6, 5, 4, 3, 2, 1]


def diff(a, b):
    return ((a[0] - b[0]) % 4, (a[1] - b[1]) % 4, (a[2] - b[2]) % 4, (a[3] - b[3]) % 2)


def plan_units():
    rank = {s: i for i, s in enumerate(ARRIVAL)}
    seen, units = {(0, 0, 0, 0)}, {i: [] for i in range(len(OFFSETS))}
    units[0].append((0, 0, False))
    pairs = sorted(itertools.combinations(range(len(OFFSETS)), 2), key=lambda p: max(rank[p[0]], rank[p[1]]))
    for p in pairs:
        a, b = sorted(p, key=lambda s: rank[s])
        d, e = diff(OFFSETS[b], OFFSETS[a]), diff(OFFSETS[a], OFFSETS[b])
        if d in seen:
            continue
        seen.update((d, e))
        units[rank[b]].append((a, b, d != e))
    assert len(seen) == 128
    return units


UNITS = plan_units()


def place():
    r, c = lax.axis_index("row"), lax.axis_index("col")
    return c % 4, r // 4, (c // 4) * 2 + (r // 2) % 2, r % 2


def device_at(x, y, z, k):
    return ((y * 2 + z % 2) * 2 + k, (z // 2) * 4 + x)


def moved(me, offset, sign):
    x, y, z, k = me
    return device_at(
        (x + sign * offset[0] + 4) % 4,
        (y + sign * offset[1] + 4) % 4,
        (z + sign * offset[2] + 4) % 4,
        (k + offset[3]) % 2,
    )


def column_of(row, lanes):
    return jnp.broadcast_to(row, (lanes, row.shape[1])).T


def kernel(
    points_ref,
    labels_ref,
    solution_ref,
    residual_ref,
    direction_ref,
    len_low_ref,
    len_high_ref,
    variances_ref,
    nugget_ref,
    coupling_ref,
    sol_out,
    res_out,
    dir_out,
    raw,
    lhs,
    rhs,
    dir_col,
    dir_row,
    acc_col,
    acc_row,
    part,
    back,
    sums_a,
    sums_b,
    load_sem,
    send_sem,
    recv_sem,
    back_send,
    back_recv,
    a_send,
    a_recv,
    b_send,
    b_recv,
):
    n = len(OFFSETS)
    me = place()
    x, y, z, k = me
    load = pltpu.make_async_copy(points_ref, raw.at[0, pl.ds(0, 64)], load_sem)
    load.start()

    group_a = [(i, zb, kk) for i in range(4) for zb in range(2) for kk in range(2)]
    group_b = [(i, zb) for i in range(4) for zb in range(2)]
    peers_a = []
    for i, zb, kk in group_a[1:]:
        peers_a.append(device_at((x + i) % 4, y, (z // 2) * 2 + (z + zb) % 2, (k + kk) % 2))
    peers_b = []
    for i, zb in group_b[1:]:
        zz = 3 - z if zb else z
        peers_b.append(device_at(x, (y + i) % 4, zz, k))

    targets = [moved(me, SOURCE[s][0], -1) for s in range(1, n)]
    owners = [moved(me, OFFSETS[s], 1) for s in range(1, n)]

    barrier = pltpu.get_barrier_semaphore()
    greet = targets + owners + peers_a + peers_b
    for d in greet:
        pl.semaphore_signal(barrier, inc=1, device_id=d, device_id_type=MESH)

    lane = lax.broadcasted_iota(jnp.int32, (1, WIDTH), 1)
    first, second = labels_ref[0].astype(F32), labels_ref[1].astype(F32)
    label = jnp.where(lane < 128, first, second)
    direction = direction_ref[...]
    sub = lax.broadcasted_iota(jnp.int32, (8, WIDTH), 0)
    raw[0, pl.ds(64, 8), :] = jnp.where(sub == 0, direction, jnp.where(sub == 1, label, 0.0))

    root = math.sqrt(LOG2E)
    scales = [
        root / column_of(len_low_ref[...], 128),
        root / column_of(len_high_ref[...], 128),
    ]
    ones = jnp.ones((1, 128), F32)
    log_var = [0.5 * LOG2E * jnp.log(ones * variances_ref[0]), 0.5 * LOG2E * jnp.log(ones * variances_ref[1])]
    log_scale = LOG2E * jnp.log(ones * coupling_ref[0])
    wide = lambda v: jnp.concatenate([v, v], axis=1)
    log_var = [wide(v) for v in log_var]
    log_scale = wide(log_scale)

    load.wait()
    pl.semaphore_wait(barrier, len(greet))

    def copy_to(s):
        return pltpu.make_async_remote_copy(
            src_ref=raw.at[SOURCE[s][1]],
            dst_ref=raw.at[s],
            send_sem=send_sem.at[s],
            recv_sem=recv_sem.at[s],
            device_id=targets[s - 1],
            device_id_type=MESH,
        )

    for s in SEND_ORDER:
        if SOURCE[s][1] == 0:
            copy_to(s).start()

    acc_col[...] = jnp.zeros_like(acc_col)
    acc_row[...] = jnp.zeros_like(acc_row)

    row16 = lax.broadcasted_iota(jnp.int32, (16, WIDTH), 0)
    zeros48 = jnp.zeros((48, WIDTH), BF16)

    def prepare(s, as_lhs, as_rhs):
        pts = raw[s, pl.ds(0, 64), :]
        d = raw[s, pl.ds(64, 1), :]
        lab = raw[s, pl.ds(65, 1), :]
        for which in range(2):
            zz = pts * wide(scales[which])
            hi = zz.astype(BF16)
            hif = hi.astype(F32)
            lo = (zz - hif).astype(BF16)
            norm = jnp.sum(hif * (hif + 2.0 * lo.astype(F32)), axis=0, keepdims=True)
            extra = lab * log_scale if which == 0 else (1.0 - lab) * MASKED
            g = log_var[which] + extra - 0.5 * norm
            g1 = g.astype(BF16).astype(F32)
            g2 = (g - g1).astype(BF16).astype(F32)
            g3 = g - g1 - g2
            if as_lhs:
                e = jnp.where(row16 == 0, g1, jnp.where(row16 == 1, g2, jnp.where(row16 == 2, g3, 0.0)))
                e = jnp.where((row16 >= 3) & (row16 < 6), 1.0, e)
                full = jnp.concatenate([hi, hi, lo, e.astype(BF16), zeros48], axis=0)
                lhs[which, s] = full.T
            if as_rhs:
                e = jnp.where(row16 == 3, g1, jnp.where(row16 == 4, g2, jnp.where(row16 == 5, g3, 0.0)))
                e = jnp.where(row16 < 3, 1.0, e)
                rhs[which, s] = jnp.concatenate([hi, lo, hi, e.astype(BF16), zeros48], axis=0)
        dir_row[s] = jnp.broadcast_to(d, (8, WIDTH))
        if as_lhs:
            dir_col[s] = column_of(d, 128)

    def unit(a, b, both):
        el = jnp.dot(lhs[0, a], rhs[0, b], preferred_element_type=F32)
        eh = jnp.dot(lhs[1, a], rhs[1, b], preferred_element_type=F32)
        m = (jnp.exp2(el) + jnp.exp2(eh)).reshape(WIDTH // 8, 8, WIDTH)
        d = dir_col[a].reshape(WIDTH // 8, 8, 128)
        acc_col[b] += jnp.sum(m * jnp.concatenate([d, d], axis=2), axis=0)
        if both:
            t = m * dir_row[b][None]
            t = t[:, :, :128] + t[:, :, 128:]
            acc_row[a] += t.reshape(WIDTH, 128)

    flat = [u for us in UNITS.values() for u in us]
    is_lhs = {a for a, _, _ in flat}
    is_rhs = {b for _, b, _ in flat}
    has_row = {a for a, _, both in flat if both}
    for i, s in enumerate(ARRIVAL):
        if s > 0:
            copy_to(s).wait_recv()
        prepare(s, s in is_lhs, s in is_rhs)
        for u in UNITS[i]:
            unit(*u)

    def total_of(s):
        t = jnp.zeros((1, WIDTH), F32)
        if s in is_rhs:
            t = t + jnp.sum(acc_col[s], axis=0, keepdims=True)
        if s in has_row:
            t = t + jnp.sum(acc_row[s].T, axis=0, keepdims=True)
        return t

    def hand_back(s):
        return pltpu.make_async_remote_copy(
            src_ref=part.at[s],
            dst_ref=back.at[s],
            send_sem=back_send.at[s],
            recv_sem=back_recv.at[s],
            device_id=owners[s - 1],
            device_id_type=MESH,
        )

    for s in range(1, n):
        part[s] = total_of(s)
    for s in range(1, n):
        hand_back(s).start()
    image = total_of(0)
    nugget_points = nugget_ref[0] + (nugget_ref[1] - nugget_ref[0]) * label
    image = image + nugget_points * direction
    residual = residual_ref[...]
    for s in range(1, n):
        hand_back(s).wait_recv()
        image = image + back[s]

    def fold(v):
        return v[:, :128] + v[:, 128:]

    mine = jnp.concatenate(
        [
            fold(residual * residual),
            fold(direction * image),
            fold(residual * image),
            fold(image * image),
            jnp.zeros((4, 128), F32),
        ],
        axis=0,
    )

    sums_a[0] = mine

    def send_a(i):
        return pltpu.make_async_remote_copy(
            src_ref=sums_a.at[0],
            dst_ref=sums_a.at[i],
            send_sem=a_send.at[i],
            recv_sem=a_recv.at[i],
            device_id=peers_a[i - 1],
            device_id_type=MESH,
        )

    for i in range(1, 16):
        send_a(i).start()
    total = mine
    for i in range(1, 16):
        send_a(i).wait_recv()
        total = total + sums_a[i]
    sums_b[0] = total

    def send_b(i):
        return pltpu.make_async_remote_copy(
            src_ref=sums_b.at[0],
            dst_ref=sums_b.at[i],
            send_sem=b_send.at[i],
            recv_sem=b_recv.at[i],
            device_id=peers_b[i - 1],
            device_id_type=MESH,
        )

    for i in range(1, 8):
        send_b(i).start()
    for i in range(1, 8):
        send_b(i).wait_recv()
        total = total + sums_b[i]

    scal = jnp.sum(total, axis=1, keepdims=True)
    old_norm, curvature, cross, image_norm = scal[0:1], scal[1:2], scal[2:3], scal[3:4]
    step = old_norm / curvature
    new_norm = old_norm - 2.0 * step * cross + step * step * image_norm
    sol_out[...] = solution_ref[...] + step * direction
    res_next = residual - step * image
    res_out[...] = res_next
    dir_out[...] = res_next + new_norm / old_norm * direction

    for s in range(1, n):
        copy_to(s).wait_send()
        hand_back(s).wait_send()
    for i in range(1, 16):
        send_a(i).wait_send()
    for i in range(1, 8):
        send_b(i).wait_send()


def body(points, labels, solution, residual, direction, len_low, len_high, variances, nugget, coupling):
    n = len(OFFSETS)
    vmem = pl.BlockSpec(memory_space=pltpu.VMEM)
    smem = pl.BlockSpec(memory_space=pltpu.SMEM)
    row = lambda v: v.reshape(1, v.shape[0])
    outs = pl.pallas_call(
        kernel,
        out_shape=[jax.ShapeDtypeStruct((1, WIDTH), F32)] * 3,
        in_specs=[pl.BlockSpec(memory_space=pl.ANY), smem, vmem, vmem, vmem, vmem, vmem, smem, smem, smem],
        out_specs=[vmem] * 3,
        scratch_shapes=[
            pltpu.VMEM((n, ROWS, WIDTH), F32),
            pltpu.VMEM((2, n, WIDTH, WIDTH), BF16),
            pltpu.VMEM((2, n, WIDTH, WIDTH), BF16),
            pltpu.VMEM((n, WIDTH, 128), F32),
            pltpu.VMEM((n, 8, WIDTH), F32),
            pltpu.VMEM((n, 8, WIDTH), F32),
            pltpu.VMEM((n, WIDTH, 128), F32),
            pltpu.VMEM((n, 1, WIDTH), F32),
            pltpu.VMEM((n, 1, WIDTH), F32),
            pltpu.VMEM((16, 8, 128), F32),
            pltpu.VMEM((8, 8, 128), F32),
            pltpu.SemaphoreType.DMA,
            pltpu.SemaphoreType.DMA((n,)),
            pltpu.SemaphoreType.DMA((n,)),
            pltpu.SemaphoreType.DMA((n,)),
            pltpu.SemaphoreType.DMA((n,)),
            pltpu.SemaphoreType.DMA((16,)),
            pltpu.SemaphoreType.DMA((16,)),
            pltpu.SemaphoreType.DMA((8,)),
            pltpu.SemaphoreType.DMA((8,)),
        ],
        compiler_params=pltpu.CompilerParams(
            collective_id=0, has_side_effects=True, vmem_limit_bytes=56 * 2**20
        ),
    )(
        points,
        labels,
        row(solution),
        row(residual),
        row(direction),
        row(len_low),
        row(len_high),
        variances,
        nugget,
        coupling,
    )
    return tuple(o.reshape(WIDTH) for o in outs)


def solution(mesh):
    both = P(("row", "col"))
    in_specs = (P(None, ("row", "col")), both, both, both, both, P(), P(), P(), P(), P())
    return jax.shard_map(body, mesh=mesh, in_specs=in_specs, out_specs=(both, both, both), check_vma=False)
```

time: 215 us -> 46.1 us (0.21); the launches traced: 212 us -> 45.9 us
  matrix products: 102 us -> 0 us
  blocking collectives: 72.4 us -> 0 us
  Pallas kernels: 0 us -> 42.1 us
  starting transfers between devices: 12.6 us -> 0 us
  other arithmetic: 7.73 us -> 0 us
  waiting for transfers between devices: 5.92 us -> 0 us
  between operations: 6.72 us -> 1.3 us
    dot_general x16 -> x0, matrix products: 102 us -> none  [the longest x4 27 us: one_block(): lax.dot_general(rows_high, part_high, dims, precision=lax.Precision.HIGHEST)]
    pallas_call x0 -> x1, Pallas kernels: none -> 42.1 us  [body(): pl.pallas_call(kernel, out_shape=[jax.ShapeDtypeStruct((1, WIDTH), F32)]...]
    psum x5 -> x0, blocking collectives: 41.4 us -> none  [one_axis_at_a_time(): return functools.reduce(lax.psum, axes, x)]
    all_gather x1 -> x0, blocking collectives: 31.1 us -> none  [in_one_piece(): whole = lax.all_gather(both, axis, axis=dim, tiled=True)]
    all_to_all x2 -> x0, starting transfers between devices: 12.6 us -> none  [the longest x1 7.33 us: copy_for_each(): lax.all_to_all(jnp.broadcast_to(x[None], (length, *x.shape)), axis, 0, 0,...]
    all_to_all x2 -> x0, waiting for transfers between devices: 5.92 us -> none  [the longest x1 5.91 us: sent_and_summed(): lax.all_to_all(blocks, axis, split_axis=0, concat_axis=0, tiled=True)]
    slice x2 -> x0, local copies, waits for them, and re-layouts: 2.63 us -> none  [the longest x1 1.31 us: body(): variances[0] * scale_factors(rows_fidelity, coupling) * sum_low]
    unnamed x13 -> x9, local copies, waits for them, and re-layouts: 0.15 us -> 2.49 us
  transfers between devices with their start and end apart: 2 -> 0, of which waited for: 1 -> 0; matrix products, arithmetic and copies ran while one was open for 3% -> 0% of each run, Pallas kernels for 0% -> 0%
where the time goes in v1:
time: 46.1 us; the launch traced here: 45.9 us
  Pallas kernels  42.1 us (91%)
  local copies, waits for them, and re-layouts  2.49 us (5%)
  between operations  1.3 us (3%)
    pallas_call x1, Pallas kernels, body(): pl.pallas_call(kernel, out_shape=[jax.ShapeDtypeStruct((1, WIDTH), F32)]...  42.1 us
    unnamed x9, local copies, waits for them, and re-layouts  2.49 us

profile of v1, /device:TPU:1, one launch (start us, length us, event | category | flops | bytes accessed | tf_op | source)
XLA Modules:
  0.0 45.9 jit_solution(13701656684586072093)
XLA Ops:
  1.3 42.1 %shard_map.121 = (f32[1,256]{1,0:T(1,128)}, f32[1,256]{1,0:T(1,128)}, f32[1,256]{1,0:T(1,128)}) custom-call(f32[64,256]{1,0:T(8,128)} %points_ref.1, s32[2]{0:T(128)} %labels_ref.1, f32[1,256]{1,0:T(1,128)} %bitcast.8, f32[1,256]{1,0:T(1,128)} %bitcast.9, f32[1,256]{1,0:T(1,128)} %bitcast.10, f32[1,64]{1,0:T(1,128)} %bitcast.14, f32[1,64]{1,0:T(1,128)} %bitcast.15, ...), custom_call_target="tpu_custom_call" | custom-call | tf_op jit(solution)/shard_map/pallas_call | solution.py:342
  43.4 0.0 copy-start.2
  43.4 0.6 %copy-done.2 = f32[1,256]{1,0:T(1,128)S(1)} copy-done((f32[1,256]{1,0:T(1,128)S(1)}, f32[1,256]{1,0:T(1,128)}, u32[]{:S(2)}) %copy-start.2) | copy-done | bytes 1048
  44.0 0.0 copy-start.1
  44.0 0.6 %copy.17 = f32[256]{0:T(256)} copy(f32[256]{0:T(256)S(1)} %bitcast.13) | data formatting | bytes 2048
  44.6 0.1 copy-done.1
  44.7 0.0 copy-start
  44.7 0.6 %copy.18 = f32[256]{0:T(256)} copy(f32[256]{0:T(256)S(1)} %bitcast.12) | data formatting | bytes 2048
  45.2 0.1 copy-done
  45.3 0.6 %copy.19 = f32[256]{0:T(256)} copy(f32[256]{0:T(256)S(1)} %bitcast.11) | data formatting | bytes 2048
Async XLA Ops:
  43.4 0.6 %copy-start.2 = (f32[1,256]{1,0:T(1,128)S(1)}, f32[1,256]{1,0:T(1,128)}, u32[]{:S(2)}) copy-start(f32[1,256]{1,0:T(1,128)} %get-tuple-element.6) | copy-start | bytes 3076
  44.0 0.6 %copy-start.1 = (f32[1,256]{1,0:T(1,128)S(1)}, f32[1,256]{1,0:T(1,128)}, u32[]{:S(2)}) copy-start(f32[1,256]{1,0:T(1,128)} %get-tuple-element.7) | copy-start | bytes 3076
  44.7 0.7 %copy-start = (f32[1,256]{1,0:T(1,128)S(1)}, f32[1,256]{1,0:T(1,128)}, u32[]{:S(2)}) copy-start(f32[1,256]{1,0:T(1,128)} %get-tuple-element.8) | copy-start | bytes 3076

commit v2 on v1

--- a/solution.py
+++ b/solution.py
@@ -17,44 +17,44 @@
 WIDTH = 256
 ROWS = 72
 
-OFFSETS = [
-    (0, 0, 0, 0),
-    (1, 0, 0, 0),
-    (0, 0, -1, 0),
-    (0, 1, 0, 1),
-    (-1, 0, 0, 1),
-    (0, -1, -1, 1),
-    (0, 1, 1, 0),
-    (-1, 0, -1, 1),
-    (-1, 1, 0, 1),
-    (1, -1, 1, 0),
-    (1, -1, 1, 1),
-    (-1, -1, -1, 1),
-    (-1, -1, 1, 0),
-    (1, 1, -1, 1),
-    (1, 1, 1, 1),
+PLAN = [
+    ((0, 0, 0, 0), (0, 0, 0, 0)),
+    ((0, 0, 0, 1), (0, 0, 0, 1)),
+    ((0, 1, 0, 0), (0, 1, 0, 0)),
+    ((-1, -1, 0, 0), (-1, -1, 0, 0)),
+    ((-1, 0, -1, 0), (-1, 0, -1, 0)),
+    ((1, 0, -1, 0), (1, 0, -1, 0)),
+    ((1, 0, 1, 0), (1, 0, 1, 0)),
+    ((-1, 0, -1, 1), (0, 0, 0, 1)),
+    ((0, 2, 0, 0), (0, 1, 0, 0)),
+    ((1, 0, -1, 1), (0, 0, 0, 1)),
+    ((1, 1, 0, 0), (1, 0, 0, 0)),
+    ((-1, 0, 2, 1), (0, 0, -1, 1)),
+    ((-1, 2, 0, 0), (0, -1, 0, 0)),
+    ((1, 0, 2, 0), (0, 0, 1, 0)),
+    ((2, -1, 0, 1), (-1, 0, 0, 1)),
+    ((-1, 2, 0, 1), (0, 0, 0, 1)),
 ]
-SOURCE = {s: (OFFSETS[s], 0) for s in range(1, len(OFFSETS))}
-SEND_ORDER = [14, 13, 12, 11, 10, 9, 8, 7, 6, 5, 4, 3, 2, 1]
-ARRIVAL = [0, 14, 13, 12, 11, 10, 9, 8, 7, 6, 5, 4, 3, 2, 1]
+OFFSETS = [row[0] for row in PLAN]
 
 
 def diff(a, b):
     return ((a[0] - b[0]) % 4, (a[1] - b[1]) % 4, (a[2] - b[2]) % 4, (a[3] - b[3]) % 2)
 
 
+HELD = [diff(block, (0, 0, 0, 0)) for block, _ in PLAN]
+ORIGIN = [HELD.index(diff(block, sender)) for block, sender in PLAN]
+
+
 def plan_units():
-    rank = {s: i for i, s in enumerate(ARRIVAL)}
-    seen, units = {(0, 0, 0, 0)}, {i: [] for i in range(len(OFFSETS))}
+    seen, units = {(0, 0, 0, 0)}, [[] for _ in OFFSETS]
     units[0].append((0, 0, False))
-    pairs = sorted(itertools.combinations(range(len(OFFSETS)), 2), key=lambda p: max(rank[p[0]], rank[p[1]]))
-    for p in pairs:
-        a, b = sorted(p, key=lambda s: rank[s])
+    for a, b in sorted(itertools.combinations(range(len(OFFSETS)), 2), key=lambda p: p[1]):
         d, e = diff(OFFSETS[b], OFFSETS[a]), diff(OFFSETS[a], OFFSETS[b])
         if d in seen:
             continue
         seen.update((d, e))
-        units[rank[b]].append((a, b, d != e))
+        units[b].append((a, b, d != e))
     assert len(seen) == 128
     return units
 
@@ -86,20 +86,19 @@
 
 
 def kernel(
-    points_ref,
-    labels_ref,
-    solution_ref,
-    residual_ref,
-    direction_ref,
-    len_low_ref,
-    len_high_ref,
-    variances_ref,
-    nugget_ref,
-    coupling_ref,
-    sol_out,
-    res_out,
-    dir_out,
+    points_in,
+    labels_in,
+    solution_in,
+    residual_in,
+    direction_in,
+    len_low_in,
+    len_high_in,
+    variances_in,
+    nugget_in,
+    coupling_in,
+    out_ref,
     raw,
+    aux,
     lhs,
     rhs,
     dir_col,
@@ -110,9 +109,20 @@
     back,
     sums_a,
     sums_b,
+    labels_ref,
+    solution_ref,
+    residual_ref,
+    direction_ref,
+    len_low_ref,
+    len_high_ref,
+    variances_ref,
+    nugget_ref,
+    coupling_ref,
     load_sem,
     send_sem,
     recv_sem,
+    aux_send,
+    aux_recv,
     back_send,
     back_recv,
     a_send,
@@ -123,9 +133,6 @@
     n = len(OFFSETS)
     me = place()
     x, y, z, k = me
-    load = pltpu.make_async_copy(points_ref, raw.at[0, pl.ds(0, 64)], load_sem)
-    load.start()
-
     group_a = [(i, zb, kk) for i in range(4) for zb in range(2) for kk in range(2)]
     group_b = [(i, zb) for i in range(4) for zb in range(2)]
     peers_a = []
@@ -136,20 +143,69 @@
         zz = 3 - z if zb else z
         peers_b.append(device_at(x, (y + i) % 4, zz, k))
 
-    targets = [moved(me, SOURCE[s][0], -1) for s in range(1, n)]
+    targets = [moved(me, PLAN[s][1], -1) for s in range(1, n)]
     owners = [moved(me, OFFSETS[s], 1) for s in range(1, n)]
 
     barrier = pltpu.get_barrier_semaphore()
-    greet = targets + owners + peers_a + peers_b
+    near = sorted({row[1] for row in PLAN[1:]})
+    greet = [moved(me, f, -1) for f in near] + [moved(me, f, 1) for f in near if diff(f, (0, 0, 0, 0)) != diff((0, 0, 0, 0), f)]
     for d in greet:
         pl.semaphore_signal(barrier, inc=1, device_id=d, device_id_type=MESH)
 
+    pairs = [
+        (labels_in, labels_ref),
+        (direction_in, direction_ref),
+        (points_in, raw.at[0]),
+        (len_low_in, len_low_ref),
+        (len_high_in, len_high_ref),
+        (coupling_in, coupling_ref),
+        (variances_in, variances_ref),
+        (nugget_in, nugget_ref),
+        (residual_in, residual_ref),
+        (solution_in, solution_ref),
+    ]
+    loads = [pltpu.make_async_copy(src, dst, load_sem.at[i]) for i, (src, dst) in enumerate(pairs)]
+    for load in loads:
+        load.start()
+    for load in loads[:2]:
+        load.wait()
     lane = lax.broadcasted_iota(jnp.int32, (1, WIDTH), 1)
-    first, second = labels_ref[0].astype(F32), labels_ref[1].astype(F32)
-    label = jnp.where(lane < 128, first, second)
+    fidelity = labels_ref[...].astype(F32)
+    label = jnp.where(lane < 128, fidelity[:, 0:1], fidelity[:, 1:2])
     direction = direction_ref[...]
-    sub = lax.broadcasted_iota(jnp.int32, (8, WIDTH), 0)
-    raw[0, pl.ds(64, 8), :] = jnp.where(sub == 0, direction, jnp.where(sub == 1, label, 0.0))
+    aux[0] = jnp.concatenate([direction, label], axis=1)
+    loads[2].wait()
+    pl.semaphore_wait(barrier, len(greet))
+
+    def copy_to(s):
+        return pltpu.make_async_remote_copy(
+            src_ref=raw.at[ORIGIN[s]],
+            dst_ref=raw.at[s],
+            send_sem=send_sem.at[s],
+            recv_sem=recv_sem.at[s],
+            device_id=targets[s - 1],
+            device_id_type=MESH,
+        )
+
+    def aux_to(s):
+        return pltpu.make_async_remote_copy(
+            src_ref=aux.at[ORIGIN[s]],
+            dst_ref=aux.at[s],
+            send_sem=aux_send.at[s],
+            recv_sem=aux_recv.at[s],
+            device_id=targets[s - 1],
+            device_id_type=MESH,
+        )
+
+    def pass_on(q):
+        for s in range(1, n):
+            if ORIGIN[s] == q:
+                copy_to(s).start()
+                aux_to(s).start()
+
+    pass_on(0)
+    for load in loads[3:]:
+        load.wait()
 
     root = math.sqrt(LOG2E)
     scales = [
@@ -157,29 +213,12 @@
         root / column_of(len_high_ref[...], 128),
     ]
     ones = jnp.ones((1, 128), F32)
-    log_var = [0.5 * LOG2E * jnp.log(ones * variances_ref[0]), 0.5 * LOG2E * jnp.log(ones * variances_ref[1])]
-    log_scale = LOG2E * jnp.log(ones * coupling_ref[0])
+    log_var = [0.5 * LOG2E * jnp.log(ones * variances_ref[0:1, 0:1]), 0.5 * LOG2E * jnp.log(ones * variances_ref[0:1, 1:2])]
+    log_scale = LOG2E * jnp.log(ones * coupling_ref[0:1, 0:1])
     wide = lambda v: jnp.concatenate([v, v], axis=1)
     log_var = [wide(v) for v in log_var]
     log_scale = wide(log_scale)
 
-    load.wait()
-    pl.semaphore_wait(barrier, len(greet))
-
-    def copy_to(s):
-        return pltpu.make_async_remote_copy(
-            src_ref=raw.at[SOURCE[s][1]],
-            dst_ref=raw.at[s],
-            send_sem=send_sem.at[s],
-            recv_sem=recv_sem.at[s],
-            device_id=targets[s - 1],
-            device_id_type=MESH,
-        )
-
-    for s in SEND_ORDER:
-        if SOURCE[s][1] == 0:
-            copy_to(s).start()
-
     acc_col[...] = jnp.zeros_like(acc_col)
     acc_row[...] = jnp.zeros_like(acc_row)
 
@@ -187,9 +226,9 @@
     zeros48 = jnp.zeros((48, WIDTH), BF16)
 
     def prepare(s, as_lhs, as_rhs):
-        pts = raw[s, pl.ds(0, 64), :]
-        d = raw[s, pl.ds(64, 1), :]
-        lab = raw[s, pl.ds(65, 1), :]
+        pts = raw[s]
+        d = aux[s][:, :WIDTH]
+        lab = aux[s][:, WIDTH:]
         for which in range(2):
             zz = pts * wide(scales[which])
             hi = zz.astype(BF16)
@@ -225,15 +264,17 @@
             t = t[:, :, :128] + t[:, :, 128:]
             acc_row[a] += t.reshape(WIDTH, 128)
 
-    flat = [u for us in UNITS.values() for u in us]
+    flat = [u for us in UNITS for u in us]
     is_lhs = {a for a, _, _ in flat}
     is_rhs = {b for _, b, _ in flat}
     has_row = {a for a, _, both in flat if both}
-    for i, s in enumerate(ARRIVAL):
+    for s in range(n):
         if s > 0:
             copy_to(s).wait_recv()
+            aux_to(s).wait_recv()
+            pass_on(s)
         prepare(s, s in is_lhs, s in is_rhs)
-        for u in UNITS[i]:
+        for u in UNITS[s]:
             unit(*u)
 
     def total_of(s):
@@ -256,10 +297,11 @@
 
     for s in range(1, n):
         part[s] = total_of(s)
-    for s in range(1, n):
-        hand_back(s).start()
+        if s > 1:
+            hand_back(s - 1).start()
     image = total_of(0)
-    nugget_points = nugget_ref[0] + (nugget_ref[1] - nugget_ref[0]) * label
+    hand_back(n - 1).start()
+    nugget_points = nugget_ref[0:1, 0:1] + (nugget_ref[0:1, 1:2] - nugget_ref[0:1, 0:1]) * label
     image = image + nugget_points * direction
     residual = residual_ref[...]
     for s in range(1, n):
@@ -320,13 +362,19 @@
     old_norm, curvature, cross, image_norm = scal[0:1], scal[1:2], scal[2:3], scal[3:4]
     step = old_norm / curvature
     new_norm = old_norm - 2.0 * step * cross + step * step * image_norm
-    sol_out[...] = solution_ref[...] + step * direction
-    res_next = residual - step * image
-    res_out[...] = res_next
-    dir_out[...] = res_next + new_norm / old_norm * direction
+    residual_next = residual - step * image
+    out_ref[...] = jnp.concatenate(
+        [
+            solution_ref[...] + step * direction,
+            residual_next,
+            residual_next + new_norm / old_norm * direction,
+        ],
+        axis=0,
+    )
 
     for s in range(1, n):
         copy_to(s).wait_send()
+        aux_to(s).wait_send()
         hand_back(s).wait_send()
     for i in range(1, 16):
         send_a(i).wait_send()
@@ -336,16 +384,28 @@
 
 def body(points, labels, solution, residual, direction, len_low, len_high, variances, nugget, coupling):
     n = len(OFFSETS)
-    vmem = pl.BlockSpec(memory_space=pltpu.VMEM)
-    smem = pl.BlockSpec(memory_space=pltpu.SMEM)
     row = lambda v: v.reshape(1, v.shape[0])
-    outs = pl.pallas_call(
+    taken = [
+        points,
+        row(labels),
+        row(solution),
+        row(residual),
+        row(direction),
+        row(len_low),
+        row(len_high),
+        row(variances),
+        row(nugget),
+        row(coupling),
+    ]
+    small = taken[1:]
+    out = pl.pallas_call(
         kernel,
-        out_shape=[jax.ShapeDtypeStruct((1, WIDTH), F32)] * 3,
-        in_specs=[pl.BlockSpec(memory_space=pl.ANY), smem, vmem, vmem, vmem, vmem, vmem, smem, smem, smem],
-        out_specs=[vmem] * 3,
+        out_shape=jax.ShapeDtypeStruct((3, WIDTH), F32),
+        in_specs=[pl.BlockSpec(memory_space=pl.ANY)] * len(taken),
+        out_specs=pl.BlockSpec(memory_space=pltpu.VMEM),
         scratch_shapes=[
-            pltpu.VMEM((n, ROWS, WIDTH), F32),
+            pltpu.VMEM((n, 64, WIDTH), F32),
+            pltpu.VMEM((n, 1, 2 * WIDTH), F32),
             pltpu.VMEM((2, n, WIDTH, WIDTH), BF16),
             pltpu.VMEM((2, n, WIDTH, WIDTH), BF16),
             pltpu.VMEM((n, WIDTH, 128), F32),
@@ -356,11 +416,9 @@
             pltpu.VMEM((n, 1, WIDTH), F32),
             pltpu.VMEM((16, 8, 128), F32),
             pltpu.VMEM((8, 8, 128), F32),
-            pltpu.SemaphoreType.DMA,
-            pltpu.SemaphoreType.DMA((n,)),
-            pltpu.SemaphoreType.DMA((n,)),
-            pltpu.SemaphoreType.DMA((n,)),
-            pltpu.SemaphoreType.DMA((n,)),
+            *[pltpu.VMEM(v.shape, v.dtype) for v in small],
+            pltpu.SemaphoreType.DMA((len(taken),)),
+            *[pltpu.SemaphoreType.DMA((n,)) for _ in range(6)],
             pltpu.SemaphoreType.DMA((16,)),
             pltpu.SemaphoreType.DMA((16,)),
             pltpu.SemaphoreType.DMA((8,)),
@@ -369,19 +427,8 @@
         compiler_params=pltpu.CompilerParams(
             collective_id=0, has_side_effects=True, vmem_limit_bytes=56 * 2**20
         ),
-    )(
-        points,
-        labels,
-        row(solution),
-        row(residual),
-        row(direction),
-        row(len_low),
-        row(len_high),
-        variances,
-        nugget,
-        coupling,
-    )
-    return tuple(o.reshape(WIDTH) for o in outs)
+    )(*taken)
+    return out[0], out[1], out[2]
 
 
 def solution(mesh):

time: 46.1 us -> 38.8 us (0.84)
  Pallas kernels: 42.1 us -> 36 us
  local copies, waits for them, and re-layouts: 2.49 us -> 1.36 us
    pallas_call x1, Pallas kernels: 42.1 us -> 36 us  [body(): pl.pallas_call(kernel, out_shape=jax.ShapeDtypeStruct((3, WIDTH), F32), i...]
    unnamed x9 -> x0, local copies, waits for them, and re-layouts: 2.49 us -> none
    slice x0 -> x1, local copies, waits for them, and re-layouts: none -> 1.36 us  [body(): return (out[0], out[1], out[2])]
where the time goes in v2:
time: 38.8 us; the launch traced here: 38.6 us
  Pallas kernels  36 us (93%)
  local copies, waits for them, and re-layouts  1.36 us (4%)
  between operations  1.29 us (3%)
    pallas_call x1, Pallas kernels, body(): pl.pallas_call(kernel, out_shape=jax.ShapeDtypeStruct((3, WIDTH), F32), i...  36 us
    slice x1, local copies, waits for them, and re-layouts, body(): return (out[0], out[1], out[2])  1.36 us

profile of v2, /device:TPU:1, one launch (start us, length us, event | category | flops | bytes accessed | tf_op | source)
XLA Modules:
  0.0 38.6 jit_solution(8966274895288828416)
XLA Ops:
  1.3 36.0 %shard_map.121 = f32[3,256]{1,0:T(4,128)} custom-call(f32[64,256]{1,0:T(8,128)} %points_in.1, s32[1,2]{1,0:T(1,128)} %bitcast.19, f32[1,256]{1,0:T(1,128)} %bitcast.13, f32[1,256]{1,0:T(1,128)} %bitcast.14, f32[1,256]{1,0:T(1,128)} %bitcast.15, f32[1,64]{1,0:T(1,128)} %bitcast.20, f32[1,64]{1,0:T(1,128)} %bitcast.21, f32[1,2]{1,0:T(1,128)} %bitcast.22, ...), custom_call_target="tpu_custom_call" | custom-call | tf_op jit(solution)/shard_map/pallas_call | solution.py:401
  37.3 1.4 %fusion = (f32[1,256]{1,0:T(1,128)}, f32[1,256]{1,0:T(1,128)}, f32[1,256]{1,0:T(1,128)}) fusion(f32[3,256]{1,0:T(4,128)} %shard_map.121), kind=kLoop, calls=%fused_computation | loop fusion | bytes 6144 | tf_op jit(solution)/shard_map/slice | solution.py:431

commit v3 on v2

--- a/solution.py
+++ b/solution.py
@@ -15,7 +15,8 @@
 LOG2E = math.log2(math.e)
 MASKED = -2000.0
 WIDTH = 256
-ROWS = 72
+PARTS = 1
+SHIFTS = (2, 1, 3, 0)
 
 PLAN = [
     ((0, 0, 0, 0), (0, 0, 0, 0)),
@@ -60,6 +61,7 @@
 
 
 UNITS = plan_units()
+STEPS = [(range(1, 7), range(0, 4)), (range(7, 11), range(4, 8)), (range(11, 13), range(8, 11)), (range(13, 16), range(11, 16))]
 
 
 def place():
@@ -74,7 +76,7 @@
 def moved(me, offset, sign):
     x, y, z, k = me
     return device_at(
-        (x + sign * offset[0] + 4) % 4,
+        (x + sign * offset[0] + 8) % 4,
         (y + sign * offset[1] + 4) % 4,
         (z + sign * offset[2] + 4) % 4,
         (k + offset[3]) % 2,
@@ -107,8 +109,8 @@
     acc_row,
     part,
     back,
-    sums_a,
-    sums_b,
+    own,
+    sums,
     labels_ref,
     solution_ref,
     residual_ref,
@@ -125,26 +127,22 @@
     aux_recv,
     back_send,
     back_recv,
-    a_send,
-    a_recv,
-    b_send,
-    b_recv,
+    own_send,
+    own_recv,
+    sums_send,
+    sums_recv,
 ):
     n = len(OFFSETS)
     me = place()
     x, y, z, k = me
-    group_a = [(i, zb, kk) for i in range(4) for zb in range(2) for kk in range(2)]
-    group_b = [(i, zb) for i in range(4) for zb in range(2)]
-    peers_a = []
-    for i, zb, kk in group_a[1:]:
-        peers_a.append(device_at((x + i) % 4, y, (z // 2) * 2 + (z + zb) % 2, (k + kk) % 2))
-    peers_b = []
-    for i, zb in group_b[1:]:
-        zz = 3 - z if zb else z
-        peers_b.append(device_at(x, (y + i) % 4, zz, k))
+    peers = []
+    for j, l, kk in list(itertools.product(range(4), range(4), range(2)))[1:]:
+        peers.append(device_at(x, (y + j) % 4, (z + l) % 4, (k + kk) % 2))
 
     targets = [moved(me, PLAN[s][1], -1) for s in range(1, n)]
-    owners = [moved(me, OFFSETS[s], 1) for s in range(1, n)]
+    lines = [
+        [moved(me, (dx + shift, dy, dz, dk), 1) for dx, dy, dz, dk in OFFSETS] for shift in range(4)
+    ]
 
     barrier = pltpu.get_barrier_semaphore()
     near = sorted({row[1] for row in PLAN[1:]})
@@ -177,12 +175,13 @@
     loads[2].wait()
     pl.semaphore_wait(barrier, len(greet))
 
-    def copy_to(s):
+    def copy_to(s, part_of):
+        rows = pl.ds(part_of * (64 // PARTS), 64 // PARTS)
         return pltpu.make_async_remote_copy(
-            src_ref=raw.at[ORIGIN[s]],
-            dst_ref=raw.at[s],
-            send_sem=send_sem.at[s],
-            recv_sem=recv_sem.at[s],
+            src_ref=raw.at[ORIGIN[s], rows],
+            dst_ref=raw.at[s, rows],
+            send_sem=send_sem.at[s, part_of],
+            recv_sem=recv_sem.at[s, part_of],
             device_id=targets[s - 1],
             device_id_type=MESH,
         )
@@ -197,13 +196,23 @@
             device_id_type=MESH,
         )
 
-    def pass_on(q):
-        for s in range(1, n):
-            if ORIGIN[s] == q:
-                copy_to(s).start()
+    onward = [[s for s in range(1, n) if ORIGIN[s] == q] for q in range(n)]
+
+    def pass_on(q, part_of):
+        for s in onward[q]:
+            copy_to(s, part_of).start()
+            if part_of == 0:
                 aux_to(s).start()
 
-    pass_on(0)
+    def take(s):
+        for part_of in range(PARTS):
+            copy_to(s, part_of).wait_recv()
+            if part_of == 0:
+                aux_to(s).wait_recv()
+            pass_on(s, part_of)
+
+    for part_of in range(PARTS):
+        pass_on(0, part_of)
     for load in loads[3:]:
         load.wait()
 
@@ -214,7 +223,7 @@
     ]
     ones = jnp.ones((1, 128), F32)
     log_var = [0.5 * LOG2E * jnp.log(ones * variances_ref[0:1, 0:1]), 0.5 * LOG2E * jnp.log(ones * variances_ref[0:1, 1:2])]
-    log_scale = LOG2E * jnp.log(ones * coupling_ref[0:1, 0:1])
+    log_scale = LOG2E * jnp.log(ones * coupling_ref[...].reshape(1, 1))
     wide = lambda v: jnp.concatenate([v, v], axis=1)
     log_var = [wide(v) for v in log_var]
     log_scale = wide(log_scale)
@@ -268,13 +277,13 @@
     is_lhs = {a for a, _, _ in flat}
     is_rhs = {b for _, b, _ in flat}
     has_row = {a for a, _, both in flat if both}
-    for s in range(n):
-        if s > 0:
-            copy_to(s).wait_recv()
-            aux_to(s).wait_recv()
-            pass_on(s)
-        prepare(s, s in is_lhs, s in is_rhs)
-        for u in UNITS[s]:
+    prepare(0, True, True)
+    for taken, ready in STEPS:
+        for s in taken:
+            take(s)
+        for s in taken:
+            prepare(s, s in is_lhs, s in is_rhs)
+        for u in sorted(u for s in ready for u in UNITS[s]):
             unit(*u)
 
     def total_of(s):
@@ -285,78 +294,75 @@
             t = t + jnp.sum(acc_row[s].T, axis=0, keepdims=True)
         return t
 
-    def hand_back(s):
+    def hand_back(s, shift):
         return pltpu.make_async_remote_copy(
             src_ref=part.at[s],
-            dst_ref=back.at[s],
-            send_sem=back_send.at[s],
-            recv_sem=back_recv.at[s],
-            device_id=owners[s - 1],
+            dst_ref=back.at[shift, s],
+            send_sem=back_send.at[shift, s],
+            recv_sem=back_recv.at[shift, s],
+            device_id=lines[shift][s],
             device_id_type=MESH,
         )
 
-    for s in range(1, n):
+    def hand_own(shift):
+        return pltpu.make_async_remote_copy(
+            src_ref=own.at[0],
+            dst_ref=own.at[shift],
+            send_sem=own_send.at[shift],
+            recv_sem=own_recv.at[shift],
+            device_id=lines[shift][0],
+            device_id_type=MESH,
+        )
+
+    residual = residual_ref[...]
+    nugget_points = nugget_ref[0:1, 0:1] + (nugget_ref[0:1, 1:2] - nugget_ref[0:1, 0:1]) * label
+    order = list(range(n - 1, 0, -1))
+    for at, s in enumerate(order):
         part[s] = total_of(s)
-        if s > 1:
-            hand_back(s - 1).start()
-    image = total_of(0)
-    hand_back(n - 1).start()
-    nugget_points = nugget_ref[0:1, 0:1] + (nugget_ref[0:1, 1:2] - nugget_ref[0:1, 0:1]) * label
-    image = image + nugget_points * direction
-    residual = residual_ref[...]
-    for s in range(1, n):
-        hand_back(s).wait_recv()
-        image = image + back[s]
+        if at > 0:
+            for shift in SHIFTS:
+                hand_back(order[at - 1], shift).start()
+    image = total_of(0) + nugget_points * direction
+    own[0] = jnp.concatenate([image, residual, direction], axis=1)
+    for shift in SHIFTS:
+        hand_back(order[-1], shift).start()
+    for shift in SHIFTS[:-1]:
+        hand_own(shift).start()
 
     def fold(v):
         return v[:, :128] + v[:, 128:]
 
-    mine = jnp.concatenate(
-        [
-            fold(residual * residual),
-            fold(direction * image),
-            fold(residual * image),
-            fold(image * image),
-            jnp.zeros((4, 128), F32),
-        ],
-        axis=0,
-    )
-
-    sums_a[0] = mine
-
-    def send_a(i):
+    total = jnp.zeros((4, 128), F32)
+    for shift in (0, 1, 3, 2):
+        if shift > 0:
+            hand_own(shift).wait_recv()
+        y_line, r_line, d_line = (own[shift][:, at * WIDTH : (at + 1) * WIDTH] for at in range(3))
+        for s in order:
+            hand_back(s, shift).wait_recv()
+            y_line = y_line + back[shift, s]
+        if shift == 0:
+            image = y_line
+        total = total + jnp.concatenate(
+            [fold(r_line * r_line), fold(d_line * y_line), fold(r_line * y_line), fold(y_line * y_line)],
+            axis=0,
+        )
+    sums[0] = total
+
+    def send_sums(i):
         return pltpu.make_async_remote_copy(
-            src_ref=sums_a.at[0],
-            dst_ref=sums_a.at[i],
-            send_sem=a_send.at[i],
-            recv_sem=a_recv.at[i],
-            device_id=peers_a[i - 1],
+            src_ref=sums.at[0],
+            dst_ref=sums.at[i],
+            send_sem=sums_send.at[i],
+            recv_sem=sums_recv.at[i],
+            device_id=peers[i - 1],
             device_id_type=MESH,
         )
 
-    for i in range(1, 16):
-        send_a(i).start()
-    total = mine
-    for i in range(1, 16):
-        send_a(i).wait_recv()
-        total = total + sums_a[i]
-    sums_b[0] = total
-
-    def send_b(i):
-        return pltpu.make_async_remote_copy(
-            src_ref=sums_b.at[0],
-            dst_ref=sums_b.at[i],
-            send_sem=b_send.at[i],
-            recv_sem=b_recv.at[i],
-            device_id=peers_b[i - 1],
-            device_id_type=MESH,
-        )
-
-    for i in range(1, 8):
-        send_b(i).start()
-    for i in range(1, 8):
-        send_b(i).wait_recv()
-        total = total + sums_b[i]
+    for i in range(31, 0, -1):
+        send_sums(i).start()
+    for i in range(1, 32):
+        send_sums(i).wait_recv()
+        total = total + sums[i]
 
     scal = jnp.sum(total, axis=1, keepdims=True)
     old_norm, curvature, cross, image_norm = scal[0:1], scal[1:2], scal[2:3], scal[3:4]
@@ -373,13 +379,15 @@
     )
 
     for s in range(1, n):
-        copy_to(s).wait_send()
+        for part_of in range(PARTS):
+            copy_to(s, part_of).wait_send()
         aux_to(s).wait_send()
-        hand_back(s).wait_send()
-    for i in range(1, 16):
-        send_a(i).wait_send()
-    for i in range(1, 8):
-        send_b(i).wait_send()
+        for shift in SHIFTS:
+            hand_back(s, shift).wait_send()
+    for shift in SHIFTS[:-1]:
+        hand_own(shift).wait_send()
+    for i in range(1, 32):
+        send_sums(i).wait_send()
 
 
 def body(points, labels, solution, residual, direction, len_low, len_high, variances, nugget, coupling):
@@ -395,7 +403,7 @@
         row(len_high),
         row(variances),
         row(nugget),
-        row(coupling),
+        coupling,
     ]
     small = taken[1:]
     out = pl.pallas_call(
@@ -413,16 +421,16 @@
             pltpu.VMEM((n, 8, WIDTH), F32),
             pltpu.VMEM((n, WIDTH, 128), F32),
             pltpu.VMEM((n, 1, WIDTH), F32),
-            pltpu.VMEM((n, 1, WIDTH), F32),
-            pltpu.VMEM((16, 8, 128), F32),
-            pltpu.VMEM((8, 8, 128), F32),
+            pltpu.VMEM((4, n, 1, WIDTH), F32),
+            pltpu.VMEM((4, 1, 3 * WIDTH), F32),
+            pltpu.VMEM((32, 4, 128), F32),
             *[pltpu.VMEM(v.shape, v.dtype) for v in small],
             pltpu.SemaphoreType.DMA((len(taken),)),
-            *[pltpu.SemaphoreType.DMA((n,)) for _ in range(6)],
-            pltpu.SemaphoreType.DMA((16,)),
-            pltpu.SemaphoreType.DMA((16,)),
-            pltpu.SemaphoreType.DMA((8,)),
-            pltpu.SemaphoreType.DMA((8,)),
+            *[pltpu.SemaphoreType.DMA((n, PARTS)) for _ in range(2)],
+            *[pltpu.SemaphoreType.DMA((n,)) for _ in range(2)],
+            *[pltpu.SemaphoreType.DMA((4, n)) for _ in range(2)],
+            *[pltpu.SemaphoreType.DMA((4,)) for _ in range(2)],
+            *[pltpu.SemaphoreType.DMA((32,)) for _ in range(2)],
         ],
         compiler_params=pltpu.CompilerParams(
             collective_id=0, has_side_effects=True, vmem_limit_bytes=56 * 2**20

time: 38.8 us -> 38 us (0.979)
  Pallas kernels: 36 us -> 35.2 us
    pallas_call x1, Pallas kernels: 36 us -> 35.2 us  [body(): pl.pallas_call(kernel, out_shape=jax.ShapeDtypeStruct((3, WIDTH), F32), i...]
where the time goes in v3:
time: 38 us; the launch traced here: 37.8 us
  Pallas kernels  35.2 us (93%)
  local copies, waits for them, and re-layouts  1.36 us (4%)
  between operations  1.29 us (3%)
    pallas_call x1, Pallas kernels, body(): pl.pallas_call(kernel, out_shape=jax.ShapeDtypeStruct((3, WIDTH), F32), i...  35.2 us
    slice x1, local copies, waits for them, and re-layouts, body(): return (out[0], out[1], out[2])  1.36 us

profile of v3, /device:TPU:1, one launch (start us, length us, event | category | flops | bytes accessed | tf_op | source)
XLA Modules:
  0.0 37.8 jit_solution(17185099768248931110)
XLA Ops:
  1.3 35.2 %shard_map.121 = f32[3,256]{1,0:T(4,128)} custom-call(f32[64,256]{1,0:T(8,128)} %points_in.1, s32[1,2]{1,0:T(1,128)} %bitcast.17, f32[1,256]{1,0:T(1,128)} %bitcast.11, f32[1,256]{1,0:T(1,128)} %bitcast.12, f32[1,256]{1,0:T(1,128)} %bitcast.13, f32[1,64]{1,0:T(1,128)} %bitcast.18, f32[1,64]{1,0:T(1,128)} %bitcast.19, f32[1,2]{1,0:T(1,128)} %bitcast.20, ...), custom_call_target="tpu_custom_call" | custom-call | tf_op jit(solution)/shard_map/pallas_call | solution.py:409
  36.5 1.4 %fusion = (f32[1,256]{1,0:T(1,128)}, f32[1,256]{1,0:T(1,128)}, f32[1,256]{1,0:T(1,128)}) fusion(f32[3,256]{1,0:T(4,128)} %shard_map.121), kind=kLoop, calls=%fused_computation | loop fusion | bytes 6144 | tf_op jit(solution)/shard_map/slice | solution.py:439

commit v4 on v3

--- a/solution.py
+++ b/solution.py
@@ -61,7 +61,7 @@
 
 
 UNITS = plan_units()
-STEPS = [(range(1, 7), range(0, 4)), (range(7, 11), range(4, 8)), (range(11, 13), range(8, 11)), (range(13, 16), range(11, 16))]
+STEPS = [((), (0,))] + [((s,), (s,)) for s in range(1, 11)] + [((11, 12), (11,)), ((13, ), (12,)), ((14,), (13,)), ((15,), (14, 15))]
 
 
 def place():
@@ -107,6 +107,7 @@
     dir_row,
     acc_col,
     acc_row,
+    row_sum,
     part,
     back,
     own,
@@ -277,6 +278,8 @@
     is_lhs = {a for a, _, _ in flat}
     is_rhs = {b for _, b, _ in flat}
     has_row = {a for a, _, both in flat if both}
+    row_left = {a: sum(u[0] == a and u[2] for u in flat) for a in has_row}
+    row_left.update({a: -1 for a in is_lhs - has_row})
     prepare(0, True, True)
     for taken, ready in STEPS:
         for s in taken:
@@ -285,13 +288,16 @@
             prepare(s, s in is_lhs, s in is_rhs)
         for u in sorted(u for s in ready for u in UNITS[s]):
             unit(*u)
+            row_left[u[0]] -= u[2]
+            if u[2] and row_left[u[0]] == 0:
+                row_sum[u[0]] = jnp.sum(acc_row[u[0]].T, axis=0, keepdims=True)
 
     def total_of(s):
         t = jnp.zeros((1, WIDTH), F32)
         if s in is_rhs:
             t = t + jnp.sum(acc_col[s], axis=0, keepdims=True)
         if s in has_row:
-            t = t + jnp.sum(acc_row[s].T, axis=0, keepdims=True)
+            t = t + row_sum[s]
         return t
 
     def hand_back(s, shift):
@@ -421,6 +427,7 @@
             pltpu.VMEM((n, 8, WIDTH), F32),
             pltpu.VMEM((n, WIDTH, 128), F32),
             pltpu.VMEM((n, 1, WIDTH), F32),
+            pltpu.VMEM((n, 1, WIDTH), F32),
             pltpu.VMEM((4, n, 1, WIDTH), F32),
             pltpu.VMEM((4, 1, 3 * WIDTH), F32),
             pltpu.VMEM((32, 4, 128), F32),

time: 38 us -> 37.3 us (0.982)
  Pallas kernels: 35.2 us -> 34.5 us
    pallas_call x1, Pallas kernels: 35.2 us -> 34.5 us  [body(): pl.pallas_call(kernel, out_shape=jax.ShapeDtypeStruct((3, WIDTH), F32), i...]
where the time goes in v4:
time: 37.3 us; the launch traced here: 37.1 us
  Pallas kernels  34.5 us (92%)
  local copies, waits for them, and re-layouts  1.36 us (4%)
  between operations  1.29 us (3%)
    pallas_call x1, Pallas kernels, body(): pl.pallas_call(kernel, out_shape=jax.ShapeDtypeStruct((3, WIDTH), F32), i...  34.5 us
    slice x1, local copies, waits for them, and re-layouts, body(): return (out[0], out[1], out[2])  1.36 us

profile of v4, /device:TPU:1, one launch (start us, length us, event | category | flops | bytes accessed | tf_op | source)
XLA Modules:
  0.0 37.1 jit_solution(14855852920033835337)
XLA Ops:
  1.3 34.5 %shard_map.121 = f32[3,256]{1,0:T(4,128)} custom-call(f32[64,256]{1,0:T(8,128)} %points_in.1, s32[1,2]{1,0:T(1,128)} %bitcast.17, f32[1,256]{1,0:T(1,128)} %bitcast.11, f32[1,256]{1,0:T(1,128)} %bitcast.12, f32[1,256]{1,0:T(1,128)} %bitcast.13, f32[1,64]{1,0:T(1,128)} %bitcast.18, f32[1,64]{1,0:T(1,128)} %bitcast.19, f32[1,2]{1,0:T(1,128)} %bitcast.20, ...), custom_call_target="tpu_custom_call" | custom-call | tf_op jit(solution)/shard_map/pallas_call | solution.py:415
  35.7 1.4 %fusion = (f32[1,256]{1,0:T(1,128)}, f32[1,256]{1,0:T(1,128)}, f32[1,256]{1,0:T(1,128)}) fusion(f32[3,256]{1,0:T(4,128)} %shard_map.121), kind=kLoop, calls=%fused_computation | loop fusion | bytes 6144 | tf_op jit(solution)/shard_map/slice | solution.py:446

commit v5 on v4

--- a/solution.py
+++ b/solution.py
@@ -278,20 +278,6 @@
     is_lhs = {a for a, _, _ in flat}
     is_rhs = {b for _, b, _ in flat}
     has_row = {a for a, _, both in flat if both}
-    row_left = {a: sum(u[0] == a and u[2] for u in flat) for a in has_row}
-    row_left.update({a: -1 for a in is_lhs - has_row})
-    prepare(0, True, True)
-    for taken, ready in STEPS:
-        for s in taken:
-            take(s)
-        for s in taken:
-            prepare(s, s in is_lhs, s in is_rhs)
-        for u in sorted(u for s in ready for u in UNITS[s]):
-            unit(*u)
-            row_left[u[0]] -= u[2]
-            if u[2] and row_left[u[0]] == 0:
-                row_sum[u[0]] = jnp.sum(acc_row[u[0]].T, axis=0, keepdims=True)
-
     def total_of(s):
         t = jnp.zeros((1, WIDTH), F32)
         if s in is_rhs:
@@ -320,9 +306,32 @@
             device_id_type=MESH,
         )
 
+    row_left = {a: sum(u[0] == a and u[2] for u in flat) for a in has_row}
+    row_left.update({a: -1 for a in is_lhs - has_row})
+    prepare(0, True, True)
+    busy = {v for t in STEPS[-1][1] for u in UNITS[t] for v in u[:2]} | {0}
+    early = [s for s in range(n - 1, 0, -1) if s not in busy]
+    for at, (taken, ready) in enumerate(STEPS):
+        if at == len(STEPS) - 1:
+            for s in early:
+                part[s] = total_of(s)
+        for s in taken:
+            take(s)
+        for s in taken:
+            prepare(s, s in is_lhs, s in is_rhs)
+        if at == len(STEPS) - 1:
+            for s in early:
+                for shift in SHIFTS:
+                    hand_back(s, shift).start()
+        for u in sorted(u for s in ready for u in UNITS[s]):
+            unit(*u)
+            row_left[u[0]] -= u[2]
+            if u[2] and row_left[u[0]] == 0:
+                row_sum[u[0]] = jnp.sum(acc_row[u[0]].T, axis=0, keepdims=True)
+
     residual = residual_ref[...]
     nugget_points = nugget_ref[0:1, 0:1] + (nugget_ref[0:1, 1:2] - nugget_ref[0:1, 0:1]) * label
-    order = list(range(n - 1, 0, -1))
+    order = [s for s in range(n - 1, 0, -1) if s not in early]
     for at, s in enumerate(order):
         part[s] = total_of(s)
         if at > 0:
@@ -343,7 +352,7 @@
         if shift > 0:
             hand_own(shift).wait_recv()
         y_line, r_line, d_line = (own[shift][:, at * WIDTH : (at + 1) * WIDTH] for at in range(3))
-        for s in order:
+        for s in early + order:
             hand_back(s, shift).wait_recv()
             y_line = y_line + back[shift, s]
         if shift == 0:

time: 37.3 us -> 37.2 us (level)
  no operation moved by 1% of the time
where the time goes in v5:
time: 37.2 us; the launch traced here: 37 us
  Pallas kernels  34.3 us (92%)
  local copies, waits for them, and re-layouts  1.36 us (4%)
  between operations  1.29 us (3%)
    pallas_call x1, Pallas kernels, body(): pl.pallas_call(kernel, out_shape=jax.ShapeDtypeStruct((3, WIDTH), F32), i...  34.3 us
    slice x1, local copies, waits for them, and re-layouts, body(): return (out[0], out[1], out[2])  1.36 us

profile of v5, /device:TPU:1, one launch (start us, length us, event | category | flops | bytes accessed | tf_op | source)
XLA Modules:
  0.0 37.0 jit_solution(14592736010664314296)
XLA Ops:
  1.3 34.3 %shard_map.121 = f32[3,256]{1,0:T(4,128)} custom-call(f32[64,256]{1,0:T(8,128)} %points_in.1, s32[1,2]{1,0:T(1,128)} %bitcast.17, f32[1,256]{1,0:T(1,128)} %bitcast.11, f32[1,256]{1,0:T(1,128)} %bitcast.12, f32[1,256]{1,0:T(1,128)} %bitcast.13, f32[1,64]{1,0:T(1,128)} %bitcast.18, f32[1,64]{1,0:T(1,128)} %bitcast.19, f32[1,2]{1,0:T(1,128)} %bitcast.20, ...), custom_call_target="tpu_custom_call" | custom-call | tf_op jit(solution)/shard_map/pallas_call | solution.py:424
  35.6 1.4 %fusion = (f32[1,256]{1,0:T(1,128)}, f32[1,256]{1,0:T(1,128)}, f32[1,256]{1,0:T(1,128)}) fusion(f32[3,256]{1,0:T(4,128)} %shard_map.121), kind=kLoop, calls=%fused_computation | loop fusion | bytes 6144 | tf_op jit(solution)/shard_map/slice | solution.py:455

commit v6 on v5

--- a/solution.py
+++ b/solution.py
@@ -449,7 +449,7 @@
             *[pltpu.SemaphoreType.DMA((32,)) for _ in range(2)],
         ],
         compiler_params=pltpu.CompilerParams(
-            collective_id=0, has_side_effects=True, vmem_limit_bytes=56 * 2**20
+            collective_id=0, has_side_effects=True, vmem_limit_bytes=28 * 2**20
         ),
     )(*taken)
     return out[0], out[1], out[2]

time: 37.2 us -> 37.2 us (level)
  local copies, waits for them, and re-layouts: 1.36 us -> 2.12 us
  Pallas kernels: 34.3 us -> 33.6 us
    unnamed x0 -> x18, local copies, waits for them, and re-layouts: none -> 1.55 us
    slice x1, local copies, waits for them, and re-layouts: 1.36 us -> 0.57 us  [body(): return (out[0], out[1], out[2])]
    pallas_call x1, Pallas kernels: 34.3 us -> 33.6 us  [body(): pl.pallas_call(kernel, out_shape=jax.ShapeDtypeStruct((3, WIDTH), F32), i...]
where the time goes in v6:
time: 37.2 us; the launch traced here: 37.1 us
  Pallas kernels  33.6 us (90%)
  local copies, waits for them, and re-layouts  2.12 us (6%)
  between operations  1.36 us (4%)
    pallas_call x1, Pallas kernels, body(): pl.pallas_call(kernel, out_shape=jax.ShapeDtypeStruct((3, WIDTH), F32), i...  33.6 us
    unnamed x18, local copies, waits for them, and re-layouts  1.55 us

profile of v6, /device:TPU:1, one launch (start us, length us, event | category | flops | bytes accessed | tf_op | source)
XLA Modules:
  0.0 37.1 jit_solution(5070448452577804851)
XLA Ops:
  1.3 0.0 copy-start.5
  1.3 0.0 copy-start.6
  1.3 0.0 copy-start.7
  1.3 0.0 copy-start.8
  1.3 0.0 copy-start.2
  1.3 0.0 copy-start.3
  1.3 0.0 copy-start.1
  1.4 0.0 copy-start.4
  1.4 0.6 %copy-done.5 = f32[64]{0:T(128)S(1)} copy-done((f32[64]{0:T(128)S(1)}, f32[64]{0:T(128)}, u32[]{:S(2)}) %copy-start.5) | copy-done | bytes 280
  1.9 0.0 copy-done.6
  2.0 0.0 copy-done.7
  2.0 0.0 copy-done.8
  2.0 0.0 copy-done.2
  2.0 0.0 copy-done.3
  2.0 0.0 copy-done.1
  2.1 0.0 copy-done.4
  2.1 0.0 copy-start
  2.1 0.8 %copy-done = f32[64,256]{1,0:T(8,128)S(1)} copy-done((f32[64,256]{1,0:T(8,128)S(1)}, f32[64,256]{1,0:T(8,128)}, u32[]{:S(2)}) %copy-start) | copy-done | bytes 65560
  2.9 33.6 %shard_map.121 = f32[3,256]{1,0:T(4,128)S(1)} custom-call(f32[64,256]{1,0:T(8,128)S(1)} %copy-done, s32[1,2]{1,0:T(1,128)S(1)} %bitcast.14, f32[1,256]{1,0:T(1,128)S(1)} %bitcast.11, f32[1,256]{1,0:T(1,128)S(1)} %bitcast.12, f32[1,256]{1,0:T(1,128)S(1)} %bitcast.13, f32[1,64]{1,0:T(1,128)S(1)} %bitcast.15, f32[1,64]{1,0:T(1,128)S(1)} %bitcast.16, ...), custom_call_target="tpu_custom_call" | custom-call | tf_op jit(solution)/shard_map/pallas_call | solution.py:424
  36.5 0.6 %fusion = (f32[1,256]{1,0:T(1,128)}, f32[1,256]{1,0:T(1,128)}, f32[1,256]{1,0:T(1,128)}) fusion(f32[3,256]{1,0:T(4,128)S(1)} %shard_map.121), kind=kLoop, calls=%fused_computation | loop fusion | bytes 6144 | tf_op jit(solution)/shard_map/slice | solution.py:455
Async XLA Ops:
  1.3 0.7 %copy-start.5 = (f32[64]{0:T(128)S(1)}, f32[64]{0:T(128)}, u32[]{:S(2)}) copy-start(f32[64]{0:T(128)} %param.15) | copy-start | bytes 772
  1.3 0.7 %copy-start.6 = (f32[64]{0:T(128)S(1)}, f32[64]{0:T(128)}, u32[]{:S(2)}) copy-start(f32[64]{0:T(128)} %param.16) | copy-start | bytes 772
  1.3 0.7 %copy-start.7 = (f32[2]{0:T(128)S(1)}, f32[2]{0:T(128)}, u32[]{:S(2)}) copy-start(f32[2]{0:T(128)} %param.17) | copy-start | bytes 28
  1.3 0.7 %copy-start.8 = (f32[2]{0:T(128)S(1)}, f32[2]{0:T(128)}, u32[]{:S(2)}) copy-start(f32[2]{0:T(128)} %param.18) | copy-start | bytes 28
  1.3 0.7 %copy-start.2 = (f32[256]{0:T(256)S(1)}, f32[256]{0:T(256)}, u32[]{:S(2)}) copy-start(f32[256]{0:T(256)} %param.13) | copy-start | bytes 3076
  1.3 0.7 %copy-start.3 = (f32[256]{0:T(256)S(1)}, f32[256]{0:T(256)}, u32[]{:S(2)}) copy-start(f32[256]{0:T(256)} %param.14) | copy-start | bytes 3076
  1.3 0.7 %copy-start.1 = (f32[256]{0:T(256)S(1)}, f32[256]{0:T(256)}, u32[]{:S(2)}) copy-start(f32[256]{0:T(256)} %param.12) | copy-start | bytes 3076
  1.4 0.7 %copy-start.4 = (s32[2]{0:T(128)S(1)}, s32[2]{0:T(128)}, u32[]{:S(2)}) copy-start(s32[2]{0:T(128)} %param.11) | copy-start | bytes 28
  2.1 0.8 %copy-start = (f32[64,256]{1,0:T(8,128)S(1)}, f32[64,256]{1,0:T(8,128)}, u32[]{:S(2)}) copy-start(f32[64,256]{1,0:T(8,128)} %points_in.1) | copy-start | bytes 196612
